TPU v7x, 32 devices: a whole 2x2x4 slice. The times are simulated.
32 devices in a mesh: row: 8 (over y, x, core), col: 4 (over z).
Axes of the slice: x: 2, y: 2, z: 4, core: 2. Of those that a mesh axis runs over, the one named last changes fastest.
Arguments:
- state: float32 [2048, 4, 1024], P('row', 'col'), may hold values from -6 to 6
- coupling: bfloat16 [2048, 4, 1024], P('row', 'col'), may hold values from -2 to 2, as said below
- coupling_t: bfloat16 [2, 2048, 4, 1024], P(None, 'row', 'col'), may hold values from -2 to 2, as said below
- factor: float32 [4, 4, 256, 256], P(None, 'col', 'row'), may hold values from -0.3 to 1.3
- cofactor: float32 [4, 4, 256, 256], P(None, 'col', 'row'), may hold values from -0.3 to 1.3
- rates: float32 [4, 4, 256], P(None, 'col'), may hold values from 0.5 to 2
Outputs:
- updated_state: float32 [2048, 4, 1024], P('row', 'col')
Inputs may be any that keep to these rules, and one draw needn't show every extreme that they name: coupling and coupling_t hold the same matrix A; its blocks A(i, k) are zero unless k > i. coupling_t holds the transposed blocks of the A in coupling.
All inputs are finite; a program needn't handle non-finite values.
Results may differ from a plain program's by a relative error of at most 0.0003.
Values may be sent and summed in bfloat16 or wider, within the bound.
A program may use at most 64 MiB of HBM per device.

v0:
```python
import jax
import jax.numpy as jnp
from jax import lax
from jax.sharding import PartitionSpec as P

STEPS = 2
HIGHEST_PRECISION = lax.Precision.HIGHEST


def broadcast(block, axis, source):
    block = jnp.where(lax.axis_index(axis) == source, block, jnp.zeros_like(block))
    return lax.psum(block, axis)


def from_behind(block, axis, distance):
    devices = range(lax.axis_size(axis))
    route = [((i - distance) % len(devices), i) for i in devices]
    return lax.ppermute(block, axis, route)


def solve_block(residual, left_p, left_q, left_e, right_p, right_q, right_e):
    middle = jnp.dot(
        left_q, residual, precision=HIGHEST_PRECISION, preferred_element_type=jnp.float32
    )
    middle = jnp.dot(
        middle, right_q.T, precision=HIGHEST_PRECISION, preferred_element_type=jnp.float32
    )
    middle = middle / (left_e[:, None] + right_e[None, :])
    product = jnp.dot(
        left_p, middle, precision=HIGHEST_PRECISION, preferred_element_type=jnp.float32
    )
    return -jnp.dot(
        product, right_p.T, precision=HIGHEST_PRECISION, preferred_element_type=jnp.float32
    )


def pick_slot(stacked, slot_index):
    return lax.dynamic_index_in_dim(stacked, slot_index, 0, keepdims=False)


def on_device(state, coupling, coupling_t, factor, cofactor, rates):
    row_count = lax.axis_size("row")
    col_count = lax.axis_size("col")
    half_rows = row_count // 2
    order_blocks = 2 * row_count
    col_slots = order_blocks // col_count
    block_size = state.shape[0]
    row_index = lax.axis_index("row")
    col_index = lax.axis_index("col")
    blocks = jnp.transpose(state.reshape(block_size, col_slots, block_size), (1, 0, 2))
    full_p, full_q = (
        lax.all_gather(factor, "row", axis=2, tiled=True),
        lax.all_gather(cofactor, "row", axis=2, tiled=True),
    )
    right_ps = full_p.reshape(col_slots, block_size, block_size)
    right_qs = full_q.reshape(col_slots, block_size, block_size)
    right_es = rates.reshape(col_slots, block_size)
    own_slot = row_index // col_count
    picked = (
        pick_slot(right_ps, own_slot),
        pick_slot(right_qs, own_slot),
        pick_slot(right_es, own_slot),
    )
    left_p, left_q, left_e = (
        broadcast(picked[0], "col", row_index % col_count),
        broadcast(picked[1], "col", row_index % col_count),
        broadcast(picked[2], "col", row_index % col_count),
    )
    upper_row = coupling.reshape(block_size, col_slots * block_size)
    lower_pair = coupling_t.reshape(2, block_size, col_slots * block_size)
    my_columns = col_index + col_count * jnp.arange(col_slots, dtype=jnp.int32)
    upper_now = upper_row
    for wave_step in range(STEPS):
        antidiag = order_blocks - 1 - wave_step
        partner = antidiag - row_index
        owner_col = partner % col_count
        slot_here = partner // col_count
        usable = row_index <= partner
        residual = pick_slot(blocks, slot_here)
        solution = solve_block(
            residual,
            left_p,
            left_q,
            left_e,
            pick_slot(right_ps, slot_here),
            pick_slot(right_qs, slot_here),
            pick_slot(right_es, slot_here),
        )
        solution = jnp.where(usable, solution, 0.0)
        written = jnp.where(usable & (col_index == owner_col), solution, residual)
        blocks = lax.dynamic_update_index_in_dim(blocks, written, slot_here, 0)
        shared = broadcast(solution, "col", owner_col)
        mirror = antidiag - my_columns
        use_row = mirror <= my_columns
        sources = jnp.clip(jnp.where(use_row, mirror, my_columns), 0, row_count - 1)
        offered = jnp.where((sources == row_index)[:, None, None], shared[None], 0.0)
        fetched = lax.psum(offered, "row")
        partner_blocks = jnp.where(use_row[:, None, None], fetched, jnp.swapaxes(fetched, 1, 2))
        if wave_step > 0:
            upper_now = from_behind(upper_row, "col", (col_count - wave_step) % col_count)
        receiver = (row_index - wave_step - half_rows) % row_count
        send_slot = jnp.where(receiver + wave_step >= row_count, 1, 0)
        send_piece = pick_slot(lower_pair, send_slot)
        lower_now = from_behind(send_piece, "row", (half_rows - wave_step) % row_count)
        upper_view = upper_now.reshape(block_size, col_slots, block_size)
        rolled = jnp.where(
            (col_index + wave_step) // col_count == 1, jnp.roll(upper_view, -1, axis=1), upper_view
        )
        lower_view = lower_now.reshape(block_size, col_slots, block_size)
        left_terms = jnp.einsum(
            "aub,ubc->uac", rolled.astype(jnp.float32), partner_blocks, precision=HIGHEST_PRECISION
        )
        right_terms = jnp.einsum(
            "ab,buc->uac", shared, lower_view.astype(jnp.float32), precision=HIGHEST_PRECISION
        )
        targets = (row_index <= my_columns) & (row_index + my_columns < antidiag)
        blocks = blocks - jnp.where(targets[:, None, None], left_terms + right_terms, 0.0)
    return jnp.transpose(blocks, (1, 0, 2)).reshape(block_size, 1, col_slots * block_size)


def solution(mesh):
    return jax.shard_map(
        on_device,
        mesh=mesh,
        in_specs=(
            P("row", "col", None),
            P("row", "col", None),
            P(None, "row", "col", None),
            P(None, "col", "row", None),
            P(None, "col", "row", None),
            P(None, "col", None),
        ),
        out_specs=P("row", "col", None),
        check_vma=False,
    )
```

profile of v0, /device:TPU:0, one launch (start us, length us, event | category | flops | bytes accessed | tf_op | source)
XLA Modules:
  0.0 328.6 jit_solution(1007737203448546680)
XLA Ops:
  6.5 0.7 all-gather.3.cloned.1.call-update
  7.3 0.0 all-gather.5.cloned.1.call-start
  7.3 0.7 all-gather.5.cloned.1.call-update
  8.0 0.0 all-reduce.15.cloned.1.call-start
  8.1 27.3 %all-gather.3.cloned.1.call-done = f32[4,1,256,256]{3,2,1,0:T(8,128)} async-done(((f32[4,1,32,256]{3,2,1,0:T(8,128)}), f32[4,1,256,256]{3,2,1,0:T(8,128)}) %all-gather.3.cloned.1.call-update) | async-done | bytes 1048592 | tf_op jit(solution)/shard_map/all_gather | solution.py:52
  35.4 1.7 select_bitcast_fusion.1
  37.0 23.6 %all-gather.5.cloned.1.call-done = f32[4,1,256,256]{3,2,1,0:T(8,128)} async-done(((f32[4,1,32,256]{3,2,1,0:T(8,128)}), f32[4,1,256,256]{3,2,1,0:T(8,128)}) %all-gather.5.cloned.1.call-update) | async-done | bytes 1048592 | tf_op jit(solution)/shard_map/all_gather | solution.py:53
  60.7 1.7 select_bitcast_fusion
  62.3 0.0 all-reduce.15.cloned.1.call-update
  62.4 0.0 all-reduce.7.cloned.1.call-start
  62.4 1.0 copy.19
  63.4 0.1 copy.51
  63.5 0.0 copy-start.15
  63.5 0.7 copy-done.15
  64.2 11.9 %psum.51 = f32[256]{0:T(256)S(1)} all-reduce(f32[256]{0:T(256)S(1)} %bitcast.106), channel_id=1, replica_groups=mesh['row'=8,'col'=4] {'col'}, use_global_device_ids=true, to_apply=%region_2.3 | all-reduce | flops 256 | bytes 2048 | tf_op jit(solution)/shard_map/psum | solution.py:12
  76.1 25.7 %all-reduce.15.cloned.1.call-done = (f32[256,256]{1,0:T(8,128)}, f32[256,256]{1,0:T(8,128)}) async-done(((f32[256,256]{1,0:T(8,128)}, f32[256,256]{1,0:T(8,128)}), (f32[256,256]{1,0:T(8,128)}, f32[256,256]{1,0:T(8,128)})) %all-reduce.15.cloned.1.call-update) | async-done | bytes 524304 | tf_op jit(solution)/shard_map/psum | solution.py:12
  101.8 1.4 fusion.24
  103.2 1.4 convolution_divide_fusion.1
  104.6 0.4 fusion.45
  105.0 0.0 copy-start.10
  105.0 1.5 bitcast_dynamic-update-slice_fusion.1
  106.5 0.0 copy-start.2
  106.5 0.8 broadcast_select_fusion.3
  107.3 0.0 all-reduce.7.cloned.1.call-update
  107.3 0.0 all-reduce.9.cloned.1.call-start
  107.4 1.1 dynamic-slice_bitcast_fusion
  108.5 1.5 collective-permute-start
  110.0 32.9 %all-reduce.7.cloned.1.call-done = f32[256,256]{0,1:T(8,128)} async-done(((f32[256,256]{0,1:T(8,128)}), f32[256,256]{0,1:T(8,128)}) %all-reduce.7.cloned.1.call-update) | async-done | bytes 262160 | tf_op jit(solution)/shard_map/psum | solution.py:12
  142.9 2.1 broadcast_select_fusion.1
  145.0 0.0 all-reduce.9.cloned.1.call-update
  145.0 0.0 all-reduce.11.cloned.1.call-start
  145.0 1.0 copy-done.12
  146.0 0.4 reshape_reshape.3
  146.4 0.2 slice.19
  146.6 0.3 slice.18
  146.9 0.7 copy.46
  147.5 0.1 copy.47
  147.7 0.2 copy.24
  147.9 54.7 %all-reduce.9.cloned.1.call-done = f32[4,256,256]{1,2,0:T(8,128)} async-done(((f32[4,256,256]{1,2,0:T(8,128)}), f32[4,256,256]{1,2,0:T(8,128)}) %all-reduce.9.cloned.1.call-update) | async-done | bytes 1048592 | tf_op jit(solution)/shard_map/psum | solution.py:97
  202.5 1.6 copy.23
  204.2 1.7 fusion.7
  206.0 0.6 fusion.4
  206.7 0.9 copy-done.11
  207.6 0.4 fusion.19
  208.0 1.4 convolution_divide_fusion
  209.4 0.4 fusion.46
  209.8 1.4 bitcast_dynamic-update-slice_fusion
  211.3 0.7 broadcast_select_fusion.2
  212.0 0.0 all-reduce.11.cloned.1.call-update
  212.0 0.0 all-reduce.13.cloned.1.call-start
  212.1 0.1 collective-permute-start.2
  212.2 0.3 copy-done.13
  212.4 3.3 collective-permute-start.1
  215.7 36.9 %all-reduce.11.cloned.1.call-done = f32[256,256]{0,1:T(8,128)} async-done(((f32[256,256]{0,1:T(8,128)}), f32[256,256]{0,1:T(8,128)}) %all-reduce.11.cloned.1.call-update) | async-done | bytes 262160 | tf_op jit(solution)/shard_map/psum | solution.py:12
  252.6 2.1 broadcast_select_fusion
  254.7 0.0 all-reduce.13.cloned.1.call-update
  254.8 0.8 copy-done.4
  255.5 0.6 slice.21
  256.2 1.3 copy.30
  257.5 0.6 convolution_bitcast_fusion
  258.1 54.2 %all-reduce.13.cloned.1.call-done = f32[4,256,256]{1,2,0:T(8,128)} async-done(((f32[4,256,256]{1,2,0:T(8,128)}), f32[4,256,256]{1,2,0:T(8,128)}) %all-reduce.13.cloned.1.call-update) | async-done | bytes 1048592 | tf_op jit(solution)/shard_map/psum | solution.py:97
  312.4 2.6 copy.29
  315.0 3.2 fusion.1
  318.2 3.6 %copy.32 = f32[256,1,1024]{2,1,0:T(1,128)} copy(f32[256,1,1024]{0,2,1:T(8,128)} %bitcast.98) | data formatting | bytes 2097152 | tf_op jit(solution)/shard_map/reshape | solution.py:118
  (37 shorter events, 0.2 us)
Async XLA Ops:
  6.5 55.9 %copy-start.9 = (f32[256,1,1024]{2,1,0:T(1,128)S(1)}, f32[256,1,1024]{2,1,0:T(1,128)}, u32[]{:S(2)}) copy-start(f32[256,1,1024]{2,1,0:T(1,128)} %param.6) | copy-start | bytes 3145732
  6.5 28.8 %all-gather.3.cloned.1.call-start = ((), (), s32[]{:S(2)}) async-start(), calls=%async_computation | async-start | bytes 1179648 | tf_op jit(solution)/shard_map/all_gather | solution.py:52
  7.3 53.4 %all-gather.5.cloned.1.call-start = ((), (), s32[]{:S(2)}) async-start(), calls=%async_computation.1 | async-start | bytes 1179648 | tf_op jit(solution)/shard_map/all_gather | solution.py:53
  8.0 93.8 %all-reduce.15.cloned.1.call-start = ((), (), s32[]{:S(2)}) async-start(), calls=%async_computation.6 | async-start | bytes 1048576 | tf_op jit(solution)/shard_map/psum | solution.py:12
  62.4 80.6 %all-reduce.7.cloned.1.call-start = ((), (), s32[]{:S(2)}) async-start(), calls=%async_computation.2 | async-start | bytes 524288 | tf_op jit(solution)/shard_map/psum | solution.py:12
  63.5 0.7 copy-start.15
  103.2 1.4 copy-start.5
  105.0 2.4 copy-start.10
  106.5 2.0 copy-start.2
  107.3 95.2 %all-reduce.9.cloned.1.call-start = ((), (), s32[]{:S(2)}) async-start(), calls=%async_computation.3 | async-start | bytes 2097152 | tf_op jit(solution)/shard_map/psum | solution.py:97
  108.5 39.2 %collective-permute-start = (bf16[256,1024]{1,0:T(8,128)(2,1)}, bf16[256,1024]{1,0:T(8,128)(2,1)S(1)}, u32[]{:S(2)}, u32[]{:S(2)}) collective-permute-start(bf16[256,1024]{1,0:T(8,128)(2,1)} %get-tuple-element.8), channel_id=1, source_target_pairs={{16,0},{20,4},{24,8},{28,12},{0,16},{4,20},{8,24},{12,28},{17,1},{... | collective-permute-start | bytes 1572872 | tf_op jit(solution)/shard_map/ppermute | solution.py:18
  145.0 1.0 copy-start.12
  145.0 107.6 %all-reduce.11.cloned.1.call-start = ((), (), s32[]{:S(2)}) async-start(), calls=%async_computation.4 | async-start | bytes 524288 | tf_op jit(solution)/shard_map/psum | solution.py:12
  202.5 1.7 copy-start
  204.2 1.8 copy-start.3
  204.2 1.8 copy-start.7
  206.6 1.0 copy-start.11
  208.0 1.4 copy-start.6
  209.8 2.3 copy-start.14
  211.3 1.1 copy-start.13
  212.0 100.3 %all-reduce.13.cloned.1.call-start = ((), (), s32[]{:S(2)}) async-start(), calls=%async_computation.5 | async-start | bytes 2097152 | tf_op jit(solution)/shard_map/psum | solution.py:97
  212.1 44.1 %collective-permute-start.2 = (bf16[256,1024]{1,0:T(8,128)(2,1)S(1)}, bf16[256,1024]{1,0:T(8,128)(2,1)}, u32[]{:S(2)}, u32[]{:S(2)}) collective-permute-start(bf16[256,1024]{1,0:T(8,128)(2,1)S(1)} %copy-done.14), channel_id=1, source_target_pairs={{20,0},{24,4},{28,8},{0,12},{4,16},{8,20},{12,24},{16,28},{21,1},{... | collective-permute-start | bytes 1572872 | tf_op jit(solution)/shard_map/ppermute | solution.py:18
  212.4 42.3 %collective-permute-start.1 = (bf16[256,1024]{1,0:T(8,128)(2,1)S(1)}, bf16[256,1024]{1,0:T(8,128)(2,1)S(1)}, u32[]{:S(2)}, u32[]{:S(2)}) collective-permute-start(bf16[256,1024]{1,0:T(8,128)(2,1)S(1)} %bitcast.105), channel_id=1, source_target_pairs={{1,0},{2,1},{3,2},{0,3},{5,4},{6,5},{7,6},{4,7},{9,8},{10,9},{11,1... | collective-permute-start | bytes 1572872 | tf_op jit(solution)/shard_map/ppermute | solution.py:18
  254.7 0.8 copy-start.4
  256.2 1.3 copy-start.8
  312.4 2.6 copy-start.1
Sparse Core Ops, SparseCore 0:
  9.2 26.0 all-gather.2
  37.3 23.3 all-gather.4
  63.1 38.7 all-reduce.14
  107.4 35.4 all-reduce.6
  145.9 56.5 all-reduce.8
  212.2 40.3 all-reduce.10
  255.7 56.5 all-reduce.12
where the time goes:
time: 329 us
  waiting for transfers between devices  257 us (78%)
  local copies, waits for them, and re-layouts  17.3 us (5%)
  matrix products  14.4 us (4%)
  between operations  14 us (4%)
  blocking collectives  11.9 us (4%)
  other arithmetic  9.03 us (3%)
  starting transfers between devices  5.04 us (2%)
    psum x2, waiting for transfers between devices, on_device(): fetched = lax.psum(offered, 'row')  109 us
    psum x3, waiting for transfers between devices, broadcast(): return lax.psum(block, axis)  95.5 us
    all_gather x1, waiting for transfers between devices, on_device(): lax.all_gather(factor, 'row', axis=2, tiled=True)  27.3 us
    all_gather x1, waiting for transfers between devices, on_device(): lax.all_gather(cofactor, 'row', axis=2, tiled=True)  23.6 us
    psum x1, blocking collectives, broadcast(): return lax.psum(block, axis)  11.9 us
  transfers between devices with their start and end apart: 10, of which 7 were waited for; matrix products, arithmetic and copies ran while one was open for 4% of the time, Pallas kernels for 0%

commit v1 on v0

--- a/solution.py
+++ b/solution.py
@@ -94,7 +94,10 @@
         use_row = mirror <= my_columns
         sources = jnp.clip(jnp.where(use_row, mirror, my_columns), 0, row_count - 1)
         offered = jnp.where((sources == row_index)[:, None, None], shared[None], 0.0)
-        fetched = lax.psum(offered, "row")
+        n_dev, fetched = (lax.axis_size("row"), offered)
+        for stride in [1 << k for k in range(n_dev.bit_length() - 1)]:
+            route_2 = [(i_2, i_2 ^ stride) for i_2 in range(n_dev)]
+            fetched = fetched + lax.ppermute(fetched, "row", route_2)
         partner_blocks = jnp.where(use_row[:, None, None], fetched, jnp.swapaxes(fetched, 1, 2))
         if wave_step > 0:
             upper_now = from_behind(upper_row, "col", (col_count - wave_step) % col_count)

time: 329 us -> 341 us (1.036)
  waiting for transfers between devices: 257 us -> 262 us
  starting transfers between devices: 5.04 us -> 9.29 us
    psum x2 -> x0, waiting for transfers between devices: 109 us -> none  [on_device(): fetched = lax.psum(offered, 'row')]
    ppermute x3, waiting for transfers between devices: 0.01 us -> 60 us  [from_behind(): return lax.ppermute(block, axis, route)]
    ppermute x0 -> x6, waiting for transfers between devices: none -> 52.8 us  [on_device(): fetched = fetched + lax.ppermute(fetched, 'row', route_2)]
    ppermute x0 -> x6, starting transfers between devices: none -> 6.29 us  [on_device(): fetched = fetched + lax.ppermute(fetched, 'row', route_2)]
    psum x2 -> x0, local copies, waits for them, and re-layouts: 4.26 us -> none  [on_device(): fetched = lax.psum(offered, 'row')]
    all_gather x1, waiting for transfers between devices: 27.3 us -> 23.6 us  [on_device(): lax.all_gather(factor, 'row', axis=2, tiled=True)]
    all_gather x1, waiting for transfers between devices: 23.6 us -> 27.3 us  [on_device(): lax.all_gather(cofactor, 'row', axis=2, tiled=True)]
    add x0 -> x6, other arithmetic: none -> 3.47 us  [on_device(): fetched = fetched + lax.ppermute(fetched, 'row', route_2)]
  transfers between devices with their start and end apart: 10 -> 14, of which waited for: 7 -> 12; matrix products, arithmetic and copies ran while one was open for 4% -> 4% of each run, Pallas kernels for 0% -> 0%
where the time goes in v1:
time: 341 us
  waiting for transfers between devices  262 us (77%)
  matrix products  17.2 us (5%)
  local copies, waits for them, and re-layouts  15.9 us (5%)
  between operations  13.6 us (4%)
  blocking collectives  11.9 us (3%)
  other arithmetic  10.8 us (3%)
  starting transfers between devices  9.29 us (3%)
    psum x3, waiting for transfers between devices, broadcast(): return lax.psum(block, axis)  96.8 us
    ppermute x3, waiting for transfers between devices, from_behind(): return lax.ppermute(block, axis, route)  60 us
    ppermute x6, waiting for transfers between devices, on_device(): fetched = fetched + lax.ppermute(fetched, 'row', route_2)  52.8 us
    all_gather x1, waiting for transfers between devices, on_device(): lax.all_gather(cofactor, 'row', axis=2, tiled=True)  27.3 us
    all_gather x1, waiting for transfers between devices, on_device(): lax.all_gather(factor, 'row', axis=2, tiled=True)  23.6 us
    psum x1, blocking collectives, broadcast(): return lax.psum(block, axis)  11.9 us
  transfers between devices with their start and end apart: 14, of which 12 were waited for; matrix products, arithmetic and copies ran while one was open for 4% of the time, Pallas kernels for 0%

profile of v1, /device:TPU:0, one launch (start us, length us, event | category | flops | bytes accessed | tf_op | source)
XLA Modules:
  0.0 340.7 jit_solution(6340757194967901209)
XLA Ops:
  6.5 0.7 all-gather.5.cloned.1.call-update
  7.3 0.7 all-gather.3.cloned.1.call-update
  8.1 27.3 %all-gather.5.cloned.1.call-done = f32[4,1,256,256]{3,2,1,0:T(8,128)} async-done(((f32[4,1,32,256]{3,2,1,0:T(8,128)}), f32[4,1,256,256]{3,2,1,0:T(8,128)}) %all-gather.5.cloned.1.call-update) | async-done | bytes 1048592 | tf_op jit(solution)/shard_map/all_gather | solution.py:53
  35.4 1.7 select_bitcast_fusion
  37.1 23.6 %all-gather.3.cloned.1.call-done = f32[4,1,256,256]{3,2,1,0:T(8,128)} async-done(((f32[4,1,32,256]{3,2,1,0:T(8,128)}), f32[4,1,256,256]{3,2,1,0:T(8,128)}) %all-gather.3.cloned.1.call-update) | async-done | bytes 1048592 | tf_op jit(solution)/shard_map/all_gather | solution.py:52
  60.7 1.7 select_bitcast_fusion.1
  62.4 0.0 all-reduce.5.cloned.1.call-start
  62.4 1.0 copy.19
  63.4 0.1 copy.51
  63.5 0.7 copy-done.12
  64.2 11.9 %psum.37 = f32[256]{0:T(256)S(1)} all-reduce(f32[256]{0:T(256)S(1)} %bitcast.100), channel_id=1, replica_groups=mesh['row'=8,'col'=4] {'col'}, use_global_device_ids=true, to_apply=%region_2.3 | all-reduce | flops 256 | bytes 2048 | tf_op jit(solution)/shard_map/psum | solution.py:12
  76.1 25.7 %all-reduce.9.cloned.1.call-done = (f32[256,256]{1,0:T(8,128)}, f32[256,256]{1,0:T(8,128)}) async-done(((f32[256,256]{1,0:T(8,128)}, f32[256,256]{1,0:T(8,128)}), (f32[256,256]{1,0:T(8,128)}, f32[256,256]{1,0:T(8,128)})) %all-reduce.9.cloned.1.call-update) | async-done | bytes 524304 | tf_op jit(solution)/shard_map/psum | solution.py:12
  101.8 1.4 fusion.22
  103.2 1.4 convolution_divide_fusion.1
  104.6 0.4 fusion.45
  105.0 1.4 bitcast_dynamic-update-slice_fusion.1
  106.4 0.8 broadcast_select_fusion.3
  107.3 35.5 %all-reduce.5.cloned.1.call-done = f32[256,256]{0,1:T(8,128)} async-done(((f32[256,256]{0,1:T(8,128)}), f32[256,256]{0,1:T(8,128)}) %all-reduce.5.cloned.1.call-update) | async-done | bytes 262160 | tf_op jit(solution)/shard_map/psum | solution.py:12
  142.9 1.2 broadcast_select_fusion.1
  144.0 0.1 collective-permute-start
  144.1 2.6 collective-permute-done
  146.8 0.2 fusion.30
  146.9 1.5 collective-permute-start.1
  148.5 23.7 %collective-permute-done.1 = f32[4,256,256]{1,2,0:T(8,128)S(1)} collective-permute-done((f32[4,256,256]{1,2,0:T(8,128)S(1)}, f32[4,256,256]{1,2,0:T(8,128)S(1)}, u32[]{:S(2)}, u32[]{:S(2)}) %collective-permute-start.1) | collective-permute-done | bytes 1048608 | tf_op jit(solution)/shard_map/ppermute | solution.py:100
  172.2 0.2 fusion.60
  172.4 1.5 collective-permute-start.2
  174.0 2.3 dynamic-slice_bitcast_fusion
  176.3 0.6 collective-permute-start.3
  176.8 0.4 reshape_reshape.3
  177.2 0.3 slice.18
  177.5 0.2 slice.19
  177.7 0.1 copy.47
  177.8 0.7 copy.46
  178.5 29.7 %collective-permute-done.3 = bf16[256,1024]{1,0:T(8,128)(2,1)} collective-permute-done((bf16[256,1024]{1,0:T(8,128)(2,1)}, bf16[256,1024]{1,0:T(8,128)(2,1)}, u32[]{:S(2)}, u32[]{:S(2)}) %collective-permute-start.3) | collective-permute-done | bytes 524320 | tf_op jit(solution)/shard_map/ppermute | solution.py:18
  208.2 1.2 copy.24
  209.4 1.6 convolution_bitcast_fusion.1
  211.1 1.4 add.172
  212.4 1.3 copy.23
  213.8 2.7 fusion.3
  216.5 0.4 fusion.17
  217.0 1.4 convolution_divide_fusion
  218.3 0.4 fusion.46
  218.7 1.4 bitcast_dynamic-update-slice_fusion
  220.1 0.7 broadcast_select_fusion.2
  220.9 35.6 %all-reduce.7.cloned.1.call-done = f32[256,256]{0,1:T(8,128)} async-done(((f32[256,256]{0,1:T(8,128)}), f32[256,256]{0,1:T(8,128)}) %all-reduce.7.cloned.1.call-update) | async-done | bytes 262160 | tf_op jit(solution)/shard_map/psum | solution.py:12
  256.5 1.2 broadcast_select_fusion
  257.6 0.1 collective-permute-start.5
  257.7 2.6 collective-permute-done.5
  260.4 0.2 fusion.31
  260.5 1.5 collective-permute-start.6
  262.1 23.7 %collective-permute-done.6 = f32[4,256,256]{1,2,0:T(8,128)S(1)} collective-permute-done((f32[4,256,256]{1,2,0:T(8,128)S(1)}, f32[4,256,256]{1,2,0:T(8,128)S(1)}, u32[]{:S(2)}, u32[]{:S(2)}) %collective-permute-start.6) | collective-permute-done | bytes 1048608 | tf_op jit(solution)/shard_map/ppermute | solution.py:100
  285.8 0.2 fusion.59
  286.0 1.5 collective-permute-start.7
  287.6 2.3 collective-permute-start.4
  289.9 10.5 %collective-permute-done.4 = bf16[256,1024]{1,0:T(8,128)(2,1)S(1)} collective-permute-done((bf16[256,1024]{1,0:T(8,128)(2,1)S(1)}, bf16[256,1024]{1,0:T(8,128)(2,1)S(1)}, u32[]{:S(2)}, u32[]{:S(2)}) %collective-permute-start.4) | collective-permute-done | bytes 524320 | tf_op jit(solution)/shard_map/ppermute | solution.py:18
  300.4 0.8 copy-done.6
  301.2 0.8 slice.20
  302.0 19.8 %collective-permute-done.8 = bf16[256,1024]{1,0:T(8,128)(2,1)} collective-permute-done((bf16[256,1024]{1,0:T(8,128)(2,1)}, bf16[256,1024]{1,0:T(8,128)(2,1)}, u32[]{:S(2)}, u32[]{:S(2)}) %collective-permute-start.8) | collective-permute-done | bytes 524320 | tf_op jit(solution)/shard_map/ppermute | solution.py:18
  321.8 1.2 copy.30
  323.0 1.6 convolution_bitcast_fusion
  324.6 1.4 add.183
  326.0 1.3 copy.29
  327.3 3.2 fusion.1
  330.5 3.6 %copy.32 = f32[256,1,1024]{2,1,0:T(1,128)} copy(f32[256,1,1024]{0,2,1:T(8,128)} %bitcast.92) | data formatting | bytes 2097152 | tf_op jit(solution)/shard_map/reshape | solution.py:121
  (42 shorter events, 0.4 us)
Async XLA Ops:
  6.5 55.9 %copy-start.8 = (f32[256,1,1024]{2,1,0:T(1,128)S(1)}, f32[256,1,1024]{2,1,0:T(1,128)}, u32[]{:S(2)}) copy-start(f32[256,1,1024]{2,1,0:T(1,128)} %param.6) | copy-start | bytes 3145732
  6.5 28.8 %all-gather.5.cloned.1.call-start = ((), (), s32[]{:S(2)}) async-start(), calls=%async_computation.1 | async-start | bytes 1179648 | tf_op jit(solution)/shard_map/all_gather | solution.py:53
  7.3 53.4 %all-gather.3.cloned.1.call-start = ((), (), s32[]{:S(2)}) async-start(), calls=%async_computation | async-start | bytes 1179648 | tf_op jit(solution)/shard_map/all_gather | solution.py:52
  8.0 93.8 %all-reduce.9.cloned.1.call-start = ((), (), s32[]{:S(2)}) async-start(), calls=%async_computation.4 | async-start | bytes 1048576 | tf_op jit(solution)/shard_map/psum | solution.py:12
  62.4 80.5 %all-reduce.5.cloned.1.call-start = ((), (), s32[]{:S(2)}) async-start(), calls=%async_computation.2 | async-start | bytes 524288 | tf_op jit(solution)/shard_map/psum | solution.py:12
  63.5 0.7 copy-start.12
  103.2 1.4 copy-start.7
  106.4 37.6 %copy-start.5 = (f32[4,256,256]{1,2,0:T(8,128)}, f32[4,256,256]{1,2,0:T(8,128)S(1)}, u32[]{:S(2)}) copy-start(f32[4,256,256]{1,2,0:T(8,128)S(1)} %get-tuple-element.12) | copy-start | bytes 3145732
  107.2 149.2 %all-reduce.7.cloned.1.call-start = ((), (), s32[]{:S(2)}) async-start(), calls=%async_computation.3 | async-start | bytes 524288 | tf_op jit(solution)/shard_map/psum | solution.py:12
  142.8 3.9 %copy-start = (f32[256,256]{0,1:T(8,128)S(1)}, f32[256,256]{0,1:T(8,128)}, u32[]{:S(2)}) copy-start(f32[256,256]{0,1:T(8,128)} %all-reduce.5.cloned.1.call-done) | copy-start | bytes 786436
  144.0 2.7 collective-permute-start
  146.9 25.3 %collective-permute-start.1 = (f32[4,256,256]{1,2,0:T(8,128)S(1)}, f32[4,256,256]{1,2,0:T(8,128)S(1)}, u32[]{:S(2)}, u32[]{:S(2)}) collective-permute-start(f32[4,256,256]{1,2,0:T(8,128)S(1)} %fusion.30), channel_id=1, source_target_pairs={{0,8},{4,12},{8,0},{12,4},{16,24},{20,28},{24,16},{28,20},{1,9},{5... | collective-permute-start | bytes 3145736 | tf_op jit(solution)/shard_map/ppermute | solution.py:100
  172.4 3.9 %copy-start.2 = (f32[4,256,256]{1,2,0:T(8,128)}, f32[4,256,256]{1,2,0:T(8,128)S(1)}, u32[]{:S(2)}) copy-start(f32[4,256,256]{1,2,0:T(8,128)S(1)} %fusion.60) | copy-start | bytes 3145732
  172.4 38.6 %collective-permute-start.2 = (f32[4,256,256]{1,2,0:T(8,128)S(1)}, f32[4,256,256]{1,2,0:T(8,128)}, u32[]{:S(2)}, u32[]{:S(2)}) collective-permute-start(f32[4,256,256]{1,2,0:T(8,128)S(1)} %fusion.60), channel_id=1, source_target_pairs={{0,16},{4,20},{8,24},{12,28},{16,0},{20,4},{24,8},{28,12},{1,17},{... | collective-permute-start | bytes 3145736 | tf_op jit(solution)/shard_map/ppermute | solution.py:100
  174.0 2.9 copy-start.10
  176.3 31.9 %collective-permute-start.3 = (bf16[256,1024]{1,0:T(8,128)(2,1)}, bf16[256,1024]{1,0:T(8,128)(2,1)}, u32[]{:S(2)}, u32[]{:S(2)}) collective-permute-start(bf16[256,1024]{1,0:T(8,128)(2,1)} %get-tuple-element.8), channel_id=1, source_target_pairs={{16,0},{20,4},{24,8},{28,12},{0,16},{4,20},{8,24},{12,28},{17,1},{... | collective-permute-start | bytes 1572872 | tf_op jit(solution)/shard_map/ppermute | solution.py:18
  209.4 1.7 copy-start.3
  213.8 2.7 copy-start.9
  256.5 3.9 %copy-start.1 = (f32[256,256]{0,1:T(8,128)S(1)}, f32[256,256]{0,1:T(8,128)}, u32[]{:S(2)}) copy-start(f32[256,256]{0,1:T(8,128)} %all-reduce.7.cloned.1.call-done) | copy-start | bytes 786436
  257.6 2.7 collective-permute-start.5
  260.5 27.0 %copy-start.11 = (bf16[256,1,1024]{2,0,1:T(8,128)(2,1)S(1)}, bf16[256,1,1024]{2,0,1:T(8,128)(2,1)}, u32[]{:S(2)}) copy-start(bf16[256,1,1024]{2,0,1:T(8,128)(2,1)} %param.7) | copy-start | bytes 1572868
  260.5 25.3 %collective-permute-start.6 = (f32[4,256,256]{1,2,0:T(8,128)S(1)}, f32[4,256,256]{1,2,0:T(8,128)S(1)}, u32[]{:S(2)}, u32[]{:S(2)}) collective-permute-start(f32[4,256,256]{1,2,0:T(8,128)S(1)} %fusion.31), channel_id=1, source_target_pairs={{0,8},{4,12},{8,0},{12,4},{16,24},{20,28},{24,16},{28,20},{1,9},{5... | collective-permute-start | bytes 3145736 | tf_op jit(solution)/shard_map/ppermute | solution.py:100
  286.0 38.6 %collective-permute-start.7 = (f32[4,256,256]{1,2,0:T(8,128)S(1)}, f32[4,256,256]{1,2,0:T(8,128)}, u32[]{:S(2)}, u32[]{:S(2)}) collective-permute-start(f32[4,256,256]{1,2,0:T(8,128)S(1)} %fusion.59), channel_id=1, source_target_pairs={{0,16},{4,20},{8,24},{12,28},{16,0},{20,4},{24,8},{28,12},{1,17},{... | collective-permute-start | bytes 3145736 | tf_op jit(solution)/shard_map/ppermute | solution.py:100
  287.6 12.8 %collective-permute-start.4 = (bf16[256,1024]{1,0:T(8,128)(2,1)S(1)}, bf16[256,1024]{1,0:T(8,128)(2,1)S(1)}, u32[]{:S(2)}, u32[]{:S(2)}) collective-permute-start(bf16[256,1024]{1,0:T(8,128)(2,1)S(1)} %bitcast.99), channel_id=1, source_target_pairs={{1,0},{2,1},{3,2},{0,3},{5,4},{6,5},{7,6},{4,7},{9,8},{10,9},{11,1... | collective-permute-start | bytes 1572872 | tf_op jit(solution)/shard_map/ppermute | solution.py:18
  289.9 31.9 %collective-permute-start.8 = (bf16[256,1024]{1,0:T(8,128)(2,1)}, bf16[256,1024]{1,0:T(8,128)(2,1)}, u32[]{:S(2)}, u32[]{:S(2)}) collective-permute-start(bf16[256,1024]{1,0:T(8,128)(2,1)} %get-tuple-element.7), channel_id=1, source_target_pairs={{20,0},{24,4},{28,8},{0,12},{4,16},{8,20},{12,24},{16,28},{21,1},{... | collective-permute-start | bytes 1572872 | tf_op jit(solution)/shard_map/ppermute | solution.py:18
  300.4 0.8 copy-start.6
  326.0 1.3 copy-start.4
Sparse Core Ops, SparseCore 0:
  9.2 26.0 all-gather.4
  37.3 23.3 all-gather.2
  63.1 38.7 all-reduce.8
  107.4 35.4 all-reduce.4
  221.0 35.4 all-reduce.6
